TPU v7x, 32 devices: a whole 2x2x4 slice. The times are simulated.
32 devices in a mesh: dp: 8 (over y, x, core), tensor: 4 (over z).
Axes of the slice: x: 2, y: 2, z: 4, core: 2. Of those that a mesh axis runs over, the one named last changes fastest.
Arguments:
- memory: bfloat16 [12288, 1280], P('dp'), may hold values from -6 to 6
- hidden: bfloat16 [12288, 2560], P('dp', 'tensor'), may hold values from -6 to 6
- grad_out: bfloat16 [12288, 2560], P('dp', 'tensor'), may hold values from -6 to 6
- key_weight: bfloat16 [1280, 2560], P('dp', 'tensor'), may hold values from -0.15625 to 0.15625
- value_weight: bfloat16 [1280, 2560], P('dp', 'tensor'), may hold values from -0.15625 to 0.15625
- row_ids: int32 [12288, 5], P('dp'), may hold values from 0 to 65535, as said below
- embed_table: float32 [65536, 256], P(('dp', 'tensor')), may hold values from -6 to 6
- first_moment: float32 [65536, 256], P(('dp', 'tensor')), may hold values from -0.6 to 0.6
- second_moment: float32 [65536, 256], P(('dp', 'tensor')), may hold values from 0.001 to 0.1
Outputs:
- key_weight_grad: float32 [1280, 2560], P('dp', 'tensor')
- value_weight_grad: float32 [1280, 2560], P('dp', 'tensor')
- new_table: float32 [65536, 256], P(('dp', 'tensor'))
- new_first: float32 [65536, 256], P(('dp', 'tensor'))
- new_second: float32 [65536, 256], P(('dp', 'tensor'))
Inputs may be any that keep to these rules, and one draw needn't show every extreme that they name: `row_ids`: the table's rows fall into 32 owners of 2048 consecutive rows each. Taking the tokens in aligned blocks of 384 consecutive tokens with all their 5 ids, at most 180 ids of one block fall in one owner's rows, and in every block some owner gets exactly 180 of them.
All inputs are finite; a program needn't handle non-finite values.
Results may differ from a plain program's by a relative error of at most 0.0043.
Values may be sent and summed in bfloat16 or wider, within the bound.
A program may use at most 128 MiB of HBM per device.

v0:
```python
import math

import jax
import jax.numpy as jnp
from jax import lax
from jax.experimental import pallas as pl
from jax.experimental.pallas import tpu as pltpu
from jax.sharding import PartitionSpec as P

beta_one = 0.9
beta_two = 0.999
learn_rate = 0.01
adam_eps = 1e-08
norm_eps = 1e-06
correct_one = 0.9999734386011124
correct_two = 0.0952078528863


def adam_update(table_grad, embed_table, first_moment, second_moment):
    new_first = beta_one * first_moment + (1.0 - beta_one) * table_grad
    new_second = beta_two * second_moment + (1.0 - beta_two) * table_grad * table_grad
    stepped = new_first / correct_one / (jnp.sqrt(new_second / correct_two) + adam_eps)
    return (embed_table - learn_rate * stepped, new_first, new_second)


f32 = jnp.float32
bf16 = jnp.bfloat16
lanes = 128
sublanes = 8


def full_spec(shape):
    return pl.BlockSpec(shape, lambda i: (0,) * len(shape))


def project_kernel(memory_ref, weights_ref, hidden_ref, grad_ref, key_ref, sums_ref):
    width = hidden_ref.shape[1]
    tile = memory_ref.shape[0]
    proj = jnp.dot(memory_ref[...], weights_ref[...], preferred_element_type=f32)
    key_proj = proj[:, :width]
    key_ref[...] = key_proj
    square = jnp.sum(key_proj * key_proj, axis=1, keepdims=True)
    cross = jnp.sum(hidden_ref[...].astype(f32) * key_proj, axis=1, keepdims=True)
    output = jnp.sum(grad_ref[...].astype(f32) * proj[:, width:], axis=1, keepdims=True)
    lane = lax.broadcasted_iota(jnp.int32, (tile, lanes), 1)
    packed = jnp.where(
        lane == 0, square, jnp.where(lane == 1, cross, jnp.where(lane == 2, output, 0.0))
    )
    sums_ref[...] = packed.T[:sublanes, :]


def grads_kernel(
    model_width, sums_ref, hidden_ref, grad_ref, key_ref, weights_ref, both_ref, piece_ref
):
    width = hidden_ref.shape[1]
    tile = hidden_ref.shape[0]
    sums = sums_ref[0]
    for part in range(1, sums_ref.shape[0]):
        sums = sums + sums_ref[part]
    root_width = math.sqrt(model_width)
    key_scale = jnp.sqrt(sums[0:1] / model_width + norm_eps)
    gate_score = sums[1:2] / (key_scale * root_width)
    gate_value = 1.0 / (1.0 + jnp.exp(-gate_score))
    gate_grad = gate_value * (1.0 - gate_value) * sums[2:3]
    hidden_factor = gate_grad / (key_scale * root_width)
    key_factor = gate_grad * (gate_score / (model_width * key_scale * key_scale))
    row = lax.broadcasted_iota(jnp.int32, (lanes, tile), 0)
    factors = jnp.where(
        row == 0, hidden_factor, jnp.where(row == 1, key_factor, gate_value)
    ).T
    key_grad = (
        factors[:, 0:1] * hidden_ref[...].astype(f32) - factors[:, 1:2] * key_ref[...]
    ).astype(bf16)
    value_grad = (factors[:, 2:3] * grad_ref[...].astype(f32)).astype(bf16)
    both_ref[:, :width] = key_grad
    both_ref[:, width:] = value_grad
    contract = (((1,), (1,)), ((), ()))
    piece_ref[...] = lax.dot_general(
        both_ref[...], weights_ref[...], contract, preferred_element_type=f32
    ).astype(bf16)


def dispatch_kernel(lookups, row_width, slot_ref, total_ref, out_ref):
    block = total_ref.shape[0]
    tile = out_ref.shape[0]
    slot = lax.broadcasted_iota(jnp.int32, (tile, block), 0) + pl.program_id(0) * tile
    rows = jnp.zeros((tile, row_width), f32)
    for lookup in range(lookups):
        hot = jnp.where(slot == slot_ref[:, lookup * block : (lookup + 1) * block], 1.0, 0.0)
        rows = rows + jnp.dot(
            hot.astype(bf16),
            total_ref[:, lookup * row_width : (lookup + 1) * row_width],
            preferred_element_type=f32,
        )
    out_ref[...] = rows.astype(bf16)


def combine_kernel(
    chunk, ids_ref, rows_ref, table_ref, first_ref, second_ref, new_table, new_first, new_second
):
    tile, row_width = table_ref.shape
    row = lax.broadcasted_iota(jnp.int32, (tile, chunk), 0) + pl.program_id(0) * tile
    table_grad = jnp.zeros((tile, row_width), f32)
    for start in range(0, rows_ref.shape[0], chunk):
        hot = jnp.where(row == ids_ref[:, start : start + chunk], 1.0, 0.0)
        table_grad = table_grad + jnp.dot(
            hot.astype(bf16), rows_ref[start : start + chunk, :], preferred_element_type=f32
        )
    new_table[...], new_first[...], new_second[...] = adam_update(
        table_grad, table_ref[...], first_ref[...], second_ref[...]
    )


def divisor(count, choices):
    return next((c for c in choices if count % c == 0), count)


def body(
    memory,
    hidden,
    grad_out,
    key_weight,
    value_weight,
    row_ids,
    embed_table,
    first_moment,
    second_moment,
):
    dp_count = lax.axis_size("dp")
    tensor_count = lax.axis_size("tensor")
    tokens, mem = memory.shape
    width = hidden.shape[1]
    model_width = width * tensor_count
    rows_dev, row_width = embed_table.shape
    lookups = row_ids.shape[1]
    block = tokens // tensor_count
    entries = block * lookups
    owners = dp_count * tensor_count
    capacity = max(2, 3 * entries // owners)
    slots = owners * capacity

    weights = lax.all_gather(
        jnp.concatenate([key_weight, value_weight], axis=1), "dp", axis=0, tiled=True
    )

    my_ids = lax.dynamic_slice_in_dim(row_ids, lax.axis_index("tensor") * block, block, 0)
    my_ids = my_ids.T.reshape(-1)
    owner_of = my_ids // rows_dev
    local_row = my_ids % rows_dev
    owner_hits = (owner_of[:, None] == jnp.arange(owners, dtype=jnp.int32)[None, :]).astype(bf16)
    earlier = (jnp.arange(entries)[None, :] < jnp.arange(entries)[:, None]).astype(bf16)
    before_counts = jnp.dot(earlier, owner_hits, preferred_element_type=f32)
    slot_rank = jnp.sum(before_counts * owner_hits.astype(f32), axis=1).astype(jnp.int32)
    slot_index = owner_of * capacity + slot_rank
    rank_hits = slot_rank[:, None] == jnp.arange(capacity, dtype=jnp.int32)[None, :]
    code = local_row + 1
    coded = jnp.concatenate(
        [
            jnp.where(rank_hits, (code // 64)[:, None], 0),
            jnp.where(rank_hits, (code % 64)[:, None], 0),
        ],
        axis=1,
    ).astype(bf16)
    sent_codes = lax.dot_general(
        owner_hits, coded, (((0,), (0,)), ((), ())), preferred_element_type=f32
    ).astype(jnp.int32)
    send_ids = sent_codes[:, :capacity] * 64 + sent_codes[:, capacity:] - 1
    got_ids = lax.all_to_all(
        send_ids, ("dp", "tensor"), split_axis=0, concat_axis=0, tiled=True
    ).reshape(1, slots)

    tile = divisor(tokens, (256, 128))
    steps = tokens // tile
    token_spec = lambda columns: pl.BlockSpec((tile, columns), lambda i: (i, 0))
    key_proj, sums = pl.pallas_call(
        project_kernel,
        grid=(steps,),
        in_specs=[token_spec(mem), full_spec((mem, 2 * width)), token_spec(width), token_spec(width)],
        out_specs=[token_spec(width), pl.BlockSpec((sublanes, tile), lambda i: (0, i))],
        out_shape=[
            jax.ShapeDtypeStruct((tokens, width), f32),
            jax.ShapeDtypeStruct((sublanes, tokens), f32),
        ],
        cost_estimate=pl.CostEstimate(
            flops=4 * tokens * mem * width, bytes_accessed=12 * tokens * width, transcendentals=0
        ),
        name="project",
    )(memory, weights, hidden, grad_out)
    all_sums = lax.all_gather(sums, "tensor", axis=0)
    both_grads, pieces = pl.pallas_call(
        lambda *refs: grads_kernel(model_width, *refs),
        grid=(steps,),
        in_specs=[
            pl.BlockSpec((tensor_count, sublanes, tile), lambda i: (0, 0, i)),
            token_spec(width),
            token_spec(width),
            token_spec(width),
            full_spec((mem, 2 * width)),
        ],
        out_specs=[token_spec(2 * width), token_spec(mem)],
        out_shape=[
            jax.ShapeDtypeStruct((tokens, 2 * width), bf16),
            jax.ShapeDtypeStruct((tokens, mem), bf16),
        ],
        cost_estimate=pl.CostEstimate(
            flops=4 * tokens * mem * width, bytes_accessed=16 * tokens * width, transcendentals=0
        ),
        name="grads",
    )(all_sums, hidden, grad_out, key_proj, weights)
    total = lax.psum_scatter(pieces, "tensor", scatter_dimension=0, tiled=True)
    weight_grads = lax.psum_scatter(
        lax.dot_general(
            memory, both_grads, (((0,), (0,)), ((), ())), preferred_element_type=f32
        ).astype(bf16),
        "dp",
        scatter_dimension=0,
        tiled=True,
    ).astype(f32)

    slot_tile = divisor(slots, (720, 960, 640, 128))
    send_rows = pl.pallas_call(
        lambda *refs: dispatch_kernel(lookups, row_width, *refs),
        grid=(slots // slot_tile,),
        in_specs=[full_spec((1, entries)), full_spec((block, mem))],
        out_specs=pl.BlockSpec((slot_tile, row_width), lambda i: (i, 0)),
        out_shape=jax.ShapeDtypeStruct((slots, row_width), bf16),
        cost_estimate=pl.CostEstimate(
            flops=2 * slots * entries * row_width, bytes_accessed=4 * slots * row_width,
            transcendentals=0,
        ),
        name="dispatch",
    )(slot_index.reshape(1, entries), total)
    got_rows = lax.all_to_all(
        send_rows.reshape(owners, capacity, row_width),
        ("dp", "tensor"),
        split_axis=0,
        concat_axis=0,
        tiled=True,
    ).reshape(slots, row_width)
    row_tile = divisor(rows_dev, (256, 128))
    row_spec = pl.BlockSpec((row_tile, row_width), lambda i: (i, 0))
    table_shape = jax.ShapeDtypeStruct((rows_dev, row_width), f32)
    chunk = divisor(slots, (1152, 960, 640, 128))
    new_table, new_first, new_second = pl.pallas_call(
        lambda *refs: combine_kernel(chunk, *refs),
        grid=(rows_dev // row_tile,),
        in_specs=[full_spec((1, slots)), full_spec((slots, row_width)), row_spec, row_spec, row_spec],
        out_specs=[row_spec] * 3,
        out_shape=[table_shape] * 3,
        cost_estimate=pl.CostEstimate(
            flops=2 * slots * rows_dev * row_width, bytes_accessed=24 * rows_dev * row_width,
            transcendentals=0,
        ),
        name="combine",
    )(got_ids, got_rows, embed_table, first_moment, second_moment)
    return (weight_grads[:, :width], weight_grads[:, width:], new_table, new_first, new_second)


def solution(mesh):
    return jax.shard_map(
        body,
        mesh=mesh,
        in_specs=(
            P("dp", None),
            P("dp", "tensor"),
            P("dp", "tensor"),
            P("dp", "tensor"),
            P("dp", "tensor"),
            P("dp", None),
            P(("dp", "tensor"), None),
            P(("dp", "tensor"), None),
            P(("dp", "tensor"), None),
        ),
        out_specs=(
            P("dp", "tensor"),
            P("dp", "tensor"),
            P(("dp", "tensor"), None),
            P(("dp", "tensor"), None),
            P(("dp", "tensor"), None),
        ),
        check_vma=False,
    )
```

profile of v0, /device:TPU:0, one launch (start us, length us, event | category | flops | bytes accessed | tf_op | source)
XLA Modules:
  0.0 278.3 jit_solution(15832017212851247458)
XLA Ops:
  7.2 0.0 all-gather.3.cloned.1.call-start
  7.2 1.8 pad_maximum_fusion
  9.0 0.0 all-gather.3.cloned.1.call-update
  9.0 0.0 reduce-scatter.5.cloned.1.call-start
  9.1 36.8 %all-gather.3.cloned.1.call-done.weights_ref.refs_4_ = bf16[1280,1280]{1,0:T(8,128)(2,1)} async-done(((bf16[160,1280]{1,0:T(8,128)(2,1)}), bf16[1280,1280]{1,0:T(8,128)(2,1)}) %all-gather.3.cloned.1.call-update) | async-done | bytes 3276816 | tf_op jit(solution)/shard_map/all_gather | solution.py:142
  45.9 10.2 %project.1 = (f32[1536,640]{1,0:T(8,128)}, f32[8,1536]{1,0:T(8,128)}) custom-call(bf16[1536,1280]{1,0:T(8,128)(2,1)} %memory_ref.1, bf16[1280,1280]{1,0:T(8,128)(2,1)} %all-gather.3.cloned.1.call-done.weights_ref.refs_4_, bf16[1536,640]{1,0:T(8,128)(2,1)} %refs_1_.1, bf16[1536,640]{1,0:T(8,128)(2,1)} %refs_2_.2), custom_call_target="tpu_custom_call" | custom-call | flops 5033164800 | bytes 11796480 | tf_op jit(solution)/shard_map/project/pallas_call | solution.py:175
  56.1 15.5 %all-gather = f32[32,1536]{1,0:T(8,128)} all-gather(f32[8,1536]{1,0:T(8,128)} %get-tuple-element.12), channel_id=2, replica_groups=mesh['dp'=8,'tensor'=4] {'tensor'}, dimensions={0}, use_global_device_ids=true | all-gather | bytes 245760 | tf_op jit(solution)/shard_map/all_gather | solution.py:189
  71.6 12.1 %grads.1 = (bf16[1536,1280]{1,0:T(8,128)(2,1)}, bf16[1536,1280]{1,0:T(8,128)(2,1)}) custom-call(f32[4,8,1536]{2,1,0:T(8,128)} %bitcast.14, bf16[1536,640]{1,0:T(8,128)(2,1)} %refs_1_.1, bf16[1536,640]{1,0:T(8,128)(2,1)} %refs_2_.2, f32[1536,640]{1,0:T(8,128)} %get-tuple-element.13.refs_3_, bf16[1280,1280]{1,0:T(8,128)(2,1)} %all-gather.3.cloned.1.call-done.weights_ref.refs_4_), custom_call_target="tpu_custom_call" | custom-call | flops 5033164800 | bytes 15728640 | tf_op jit(solution)/shard_map/grads/pallas_call | solution.py:190
  83.7 0.0 reduce-scatter.5.cloned.1.call-update
  83.7 0.7 dynamic-slice_bitcast_fusion
  84.5 1.4 fusion.7
  85.9 1.4 select_convert_fusion.1
  87.3 0.6 fusion.8
  87.9 0.1 fusion.15
  88.0 0.7 copy.18
  88.6 3.7 %all-to-all-start = ((s32[32,1,180]{2,1,0:T(1,128)}), s32[32,1,180]{2,1,0:T(1,128)S(1)}, u32[]{:S(2)}, u32[]{:S(2)}) async-start(s32[32,1,180]{2,1,0:T(1,128)} %copy.18), calls=%async_computation | async-start | bytes 65536 | tf_op jit(solution)/shard_map/all_to_all | solution.py:168
  92.4 0.6 reshape_add_fusion.refs_0_
  93.0 63.1 %reduce-scatter.5.cloned.1.call-done.refs_1_ = bf16[384,1280]{1,0:T(8,128)(2,1)} async-done(((bf16[1536,1280]{1,0:T(8,128)(2,1)}), bf16[384,1280]{1,0:T(8,128)(2,1)}) %reduce-scatter.5.cloned.1.call-update) | async-done | bytes 983056 | tf_op jit(solution)/shard_map/reduce_scatter | solution.py:210
  156.1 10.9 %dispatch.1 = bf16[5760,256]{1,0:T(8,128)(2,1)} custom-call(s32[1,1920]{1,0:T(1,128)} %reshape_add_fusion.refs_0_, bf16[384,1280]{1,0:T(8,128)(2,1)} %reduce-scatter.5.cloned.1.call-done.refs_1_), custom_call_target="tpu_custom_call" | custom-call | flops 5662310400 | bytes 5898240 | tf_op jit(solution)/shard_map/dispatch/pallas_call | solution.py:221
  167.0 5.3 %reshape.201 = bf16[32,180,256]{2,1,0:T(8,128)(2,1)} reshape(bf16[5760,256]{1,0:T(8,128)(2,1)} %dispatch.1) | data formatting | bytes 5898240 | tf_op jit(solution)/shard_map/reshape | solution.py:234
  172.3 0.0 all-to-all-done
  172.3 5.1 %all-to-all-start.1 = ((bf16[32,180,256]{2,1,0:T(8,128)(2,1)}), bf16[32,180,256]{2,1,0:T(8,128)(2,1)S(1)}, u32[]{:S(2)}, u32[]{:S(2)}) async-start(bf16[32,180,256]{2,1,0:T(8,128)(2,1)} %reshape.201), calls=%async_computation.2 | async-start | bytes 6029312 | tf_op jit(solution)/shard_map/all_to_all | solution.py:233
  177.4 0.0 reduce-scatter.7.cloned.1.call-start
  177.5 9.5 %fusion.1 = bf16[1280,1280]{0,1:T(8,128)(2,1)} fusion(bf16[1536,1280]{1,0:T(8,128)(2,1)} %get-tuple-element.14, bf16[1536,1280]{1,0:T(8,128)(2,1)} %memory_ref.1), kind=kOutput, calls=%fused_computation.3 | convolution fusion | flops 5034803200 | bytes 11141120 | tf_op jit(solution)/shard_map/dot_general | solution.py:212
  187.0 5.7 %copy.21 = bf16[1280,1280]{1,0:T(8,128)(2,1)} copy(bf16[1280,1280]{0,1:T(8,128)(2,1)} %fusion.1) | data formatting | bytes 6553600
  192.6 0.0 reduce-scatter.7.cloned.1.call-update
  192.6 0.1 reduce
  192.7 0.8 reshape.199.refs_0_
  193.5 54.4 %reduce-scatter.7.cloned.1.call-done = bf16[160,1280]{1,0:T(8,128)(2,1)} async-done(((bf16[1280,1280]{1,0:T(8,128)(2,1)}), bf16[160,1280]{1,0:T(8,128)(2,1)}) %reduce-scatter.7.cloned.1.call-update) | async-done | bytes 409616
  247.9 2.1 copy.22
  250.0 2.2 fusion.22
  252.2 2.0 copy.19
  254.3 2.0 copy.20
  256.3 0.0 all-to-all-done.1
  256.3 2.3 reshape.202.refs_1_
  258.6 13.1 %combine.1 = (f32[2048,256]{1,0:T(8,128)}, f32[2048,256]{1,0:T(8,128)}, f32[2048,256]{1,0:T(8,128)}) custom-call(s32[1,5760]{1,0:T(1,128)} %reshape.199.refs_0_, bf16[5760,256]{1,0:T(8,128)(2,1)} %reshape.202.refs_1_, f32[2048,256]{1,0:T(8,128)} %refs_2_.3, f32[2048,256]{1,0:T(8,128)} %refs_3_.1, f32[2048,256]{1,0:T(8,128)} %refs_4_.1), custom_call_target="tpu_custom_call" | custom-call | flops 6039797760 | bytes 12582912 | tf_op jit(solution)/shard_map/combine/pallas_call | solution.py:244
  (4 shorter events, 0.0 us)
Async XLA Ops:
  7.2 38.8 %all-gather.3.cloned.1.call-start = ((), (), s32[]{:S(2)}) async-start(), calls=%async_computation.4 | async-start | bytes 3686400 | tf_op jit(solution)/shard_map/all_gather | solution.py:142
  9.0 147.1 %reduce-scatter.5.cloned.1.call-start = ((), (), s32[]{:S(2)}) async-start(), calls=%async_computation.5 | async-start | bytes 4915200 | tf_op jit(solution)/shard_map/reduce_scatter | solution.py:210
  88.6 83.7 %all-to-all-start = ((s32[32,1,180]{2,1,0:T(1,128)}), s32[32,1,180]{2,1,0:T(1,128)S(1)}, u32[]{:S(2)}, u32[]{:S(2)}) async-start(s32[32,1,180]{2,1,0:T(1,128)} %copy.18), calls=%async_computation | async-start | bytes 65536 | tf_op jit(solution)/shard_map/all_to_all | solution.py:168
  172.3 84.0 %all-to-all-start.1 = ((bf16[32,180,256]{2,1,0:T(8,128)(2,1)}), bf16[32,180,256]{2,1,0:T(8,128)(2,1)S(1)}, u32[]{:S(2)}, u32[]{:S(2)}) async-start(bf16[32,180,256]{2,1,0:T(8,128)(2,1)} %reshape.201), calls=%async_computation.2 | async-start | bytes 6029312 | tf_op jit(solution)/shard_map/all_to_all | solution.py:233
  177.4 70.5 %reduce-scatter.7.cloned.1.call-start = ((), (), s32[]{:S(2)}) async-start(), calls=%async_computation.6 | async-start | bytes 3686400
Sparse Core Ops, SparseCore 0:
  10.4 35.4 all-gather.2
  83.8 72.2 reduce-scatter.4
  192.8 55.1 reduce-scatter.6
where the time goes:
time: 279 us; the launch traced here: 278 us
  waiting for transfers between devices  154 us (55%)
  Pallas kernels  46.3 us (17%)
  local copies, waits for them, and re-layouts  23.8 us (9%)
  blocking collectives  15.5 us (6%)
  between operations  13.8 us (5%)
  matrix products  11.5 us (4%)
  starting transfers between devices  8.94 us (3%)
  other arithmetic  4.05 us (1%)
    reduce_scatter x1, waiting for transfers between devices, body(): total = lax.psum_scatter(pieces, 'tensor', scatter_dimension=0, tiled=True)  63.1 us
    unnamed x4, waiting for transfers between devices  54.5 us
    all_gather x1, waiting for transfers between devices, body(): lax.all_gather(jnp.concatenate([key_weight, value_weight], axis=1), 'dp',...  36.8 us
    all_gather x1, blocking collectives, body(): all_sums = lax.all_gather(sums, 'tensor', axis=0)  15.5 us
    pallas_call x1, Pallas kernels, body(): pl.pallas_call(lambda *refs: combine_kernel(chunk, *refs), grid=(rows_dev...  13.1 us
    unnamed x6, local copies, waits for them, and re-layouts  12.6 us
    pallas_call x1, Pallas kernels, body(): pl.pallas_call(lambda *refs: grads_kernel(model_width, *refs), grid=(step...  12.1 us
    pallas_call x1, Pallas kernels, body(): pl.pallas_call(lambda *refs: dispatch_kernel(lookups, row_width, *refs),...  10.9 us
  transfers between devices with their start and end apart: 5, of which 3 were waited for; matrix products, arithmetic and copies ran while one was open for 13% of the time, Pallas kernels for 4%

commit v1 on v0

v1 whole, which is shorter than its diff:
```python
import math

import jax
import jax.numpy as jnp
from jax import lax
from jax.experimental import pallas as pl
from jax.experimental.pallas import tpu as pltpu
from jax.sharding import PartitionSpec as P

beta_one = 0.9
beta_two = 0.999
learn_rate = 0.01
adam_eps = 1e-08
norm_eps = 1e-06
correct_one = 0.9999734386011124
correct_two = 0.0952078528863


f32 = jnp.float32
bf16 = jnp.bfloat16
lanes = 128
sublanes = 8


MESH = pl.DeviceIdType.MESH
contract_lanes = (((1,), (1,)), ((), ()))
contract_rows = (((0,), (0,)), ((), ()))


def divisor(count, choices):
    return next((c for c in choices if count % c == 0), count)


def step_kernel(
    plan,
    memory_hbm,
    hidden_hbm,
    grad_hbm,
    key_w_hbm,
    value_w_hbm,
    ids_hbm,
    key_out,
    value_out,
    table_out,
    mem_s,
    hid_s,
    grd_s,
    w_s,
    w_slab_s,
    key_s,
    both_s,
    part_s,
    in_s,
    mid_s,
    total_s,
    sums_s,
    ids_s,
    slot_s,
    own_s,
    gid_s,
    send_s,
    got_s,
    wg_s,
    wg_slab_s,
    pair_s,
    half_s,
    local_sem,
    ids_ssem,
    ids_rsem,
    ag_ssem,
    ag_rsem,
    dd_ssem,
    dd_rsem,
    sum_ssem,
    sum_rsem,
    part_ssem,
    part_rsem,
    mid_ssem,
    mid_rsem,
    total_ssem,
    total_rsem,
    row_ssem,
    row_rsem,
    pair_ssem,
    pair_rsem,
    half_ssem,
    half_rsem,
):
    dp_count, t_count = plan["dp"], plan["tensor"]
    tokens, mem, width = plan["tokens"], plan["mem"], plan["width"]
    shard, cap, rows_dev = plan["shard"], plan["cap"], plan["rows_dev"]
    lookups, row_width = plan["lookups"], plan["row_width"]
    blocks, block, tile, chunk = t_count, plan["block"], plan["tile"], plan["chunk"]
    aligned = plan["aligned"]
    model_width = width * t_count
    entries = block * lookups
    chips = dp_count // 2
    bits = chips.bit_length() - 1
    chunks = tokens // chunk
    tiles = tokens // tile
    per_tile = tile // chunk
    wide = plan["wide"]
    wides = tokens // wide
    per_wide = wide // tile
    per_block = block // chunk
    slots = dp_count * cap

    me = lax.axis_index("dp")
    z = lax.axis_index("tensor")
    core = me % 2
    chip = me // 2
    partner = chip * 2 + 1 - core
    is_mid = jnp.logical_and(z > 0, z < t_count - 1)
    is_end = jnp.logical_or(z == 0, z == t_count - 1)
    mate = z + 1 - 2 * (z % 2)
    other = t_count - 1 - z

    def remote(src, dst, ssem, rsem, dev_dp, dev_z):
        return pltpu.make_async_remote_copy(
            src_ref=src,
            dst_ref=dst,
            send_sem=ssem,
            recv_sem=rsem,
            device_id=(dev_dp, dev_z),
            device_id_type=MESH,
        )

    def slab_of(flat, stacked, index):
        if aligned:
            return flat.at[pl.ds(pl.multiple_of(index * shard, shard), shard)]
        return stacked.at[index]

    def w_slab(index):
        return slab_of(w_s, w_slab_s, index)

    def wg_slab(index):
        return slab_of(wg_s, wg_slab_s, index)

    own = w_slab(me)
    local = [
        pltpu.make_async_copy(key_w_hbm, own.at[:, :width], local_sem.at[0]),
        pltpu.make_async_copy(value_w_hbm, own.at[:, width:], local_sem.at[1]),
        pltpu.make_async_copy(ids_hbm, ids_s.at[me], local_sem.at[2]),
        pltpu.make_async_copy(memory_hbm, mem_s, local_sem.at[3]),
        pltpu.make_async_copy(hidden_hbm, hid_s, local_sem.at[4]),
        pltpu.make_async_copy(grad_hbm, grd_s, local_sem.at[5]),
    ]
    for copy in local:
        copy.start()

    barrier = pltpu.get_barrier_semaphore()
    for i in range(1, dp_count):
        pl.semaphore_signal(
            barrier, inc=1, device_id=((me + i) % dp_count, z), device_id_type=MESH
        )
    for i in range(1, t_count):
        pl.semaphore_signal(
            barrier, inc=1, device_id=(me, (z + i) % t_count), device_id_type=MESH
        )
    pl.semaphore_wait(barrier, dp_count - 1 + t_count - 1)

    def flip(x, s):
        a, b = 1 << s, 1 << (bits - 1 - s)
        f0 = x + a * (1 - 2 * ((x // a) % 2))
        f1 = x + b * (1 - 2 * ((x // b) % 2))
        return f0 * (1 - core) + f1 * core

    have = [chip]
    for s in range(bits):
        have = have + [flip(x, s) for x in have]

    def gather_copy(s, k):
        at = (1 << s) + k
        ref = w_slab(have[k] * 2 + core)
        return remote(ref, ref, ag_ssem.at[at], ag_rsem.at[at], flip(chip, s) * 2 + core, z)

    def across_copy(k):
        ref = w_slab(have[k] * 2 + core)
        return remote(ref, ref, dd_ssem.at[k], dd_rsem.at[k], partner, z)

    def ids_copy(i):
        ref = ids_s.at[me]
        return remote(ref, ref, ids_ssem.at[i], ids_rsem.at[i], (me + i) % dp_count, z)

    local[0].wait()
    local[1].wait()
    across_copy(0).start()
    for s in range(bits):
        if s:
            gather_copy(s - 1, 0).wait_send()
        gather_copy(s, 0).start()
    local[2].wait()

    upper = (
        lax.broadcasted_iota(jnp.int32, (lanes, lanes), 0)
        <= lax.broadcasted_iota(jnp.int32, (lanes, lanes), 1)
    )
    upper = jnp.where(upper, 1.0, 0.0).astype(bf16)

    def running(hits):
        carry = jnp.zeros((hits.shape[0], 1), f32)
        parts = []
        for start in range(0, entries, lanes):
            part = carry + jnp.dot(
                hits[:, start : start + lanes].astype(bf16), upper, preferred_element_type=f32
            )
            carry = part[:, lanes - 1 : lanes]
            parts.append(part)
        return jnp.concatenate(parts, axis=1)

    dest = lax.broadcasted_iota(jnp.int32, (dp_count, entries), 0)
    for b in range(blocks):
        owner_of = lax.div(ids_s[me, b : b + 1, :], jnp.int32(rows_dev))
        hits = jnp.where(owner_of == dest * t_count + z, 1.0, 0.0)
        ranked = hits * (running(hits) + (dest * cap).astype(f32))
        slot_s[b : b + 1, :] = jnp.sum(ranked, axis=0, keepdims=True).astype(jnp.int32) - 1

    def forward(k):
        s = k.bit_length() - 1
        gather_copy(s, k - (1 << s)).wait_recv()
        for later in range(s + 1, bits):
            gather_copy(later, k).start()
        across_copy(k).start()

    for k in range(1, chips):
        forward(k)
    for i in range(1, dp_count):
        ids_copy(i).start()

    def own_slots(j, carry):
        owner_of = lax.div(ids_s[j], jnp.int32(rows_dev))
        hits = jnp.where(owner_of == me * t_count + z, 1.0, 0.0)
        own_s[j] = (hits * running(hits)).astype(jnp.int32) - 1
        return carry

    id_tiles = slots // lanes
    id_parts = divisor(id_tiles, (4, 3, 2))
    id_each = id_tiles // id_parts

    def own_ids(b, part):
        for start in range(part * id_each * lanes, (part + 1) * id_each * lanes, lanes):
            first = start // cap
            last = (start + lanes - 1) // cap
            found = jnp.zeros((sublanes, lanes), f32)
            for j in range(first, last + 1):
                local_row = lax.rem(ids_s[j, pl.ds(b, 1), :], jnp.int32(rows_dev)) + 1
                row = lax.broadcasted_iota(jnp.int32, (sublanes, entries), 0)
                codes = jnp.where(
                    row == 0,
                    lax.div(local_row, jnp.int32(64)),
                    jnp.where(row == 1, lax.rem(local_row, jnp.int32(64)), 0),
                )
                slot = lax.broadcasted_iota(jnp.int32, (lanes, entries), 0) + (start - j * cap)
                hot = jnp.where(slot == own_s[j, pl.ds(b, 1), :], 1.0, 0.0)
                hot = jnp.where(slot < 0, 0.0, hot)
                found = found + lax.dot_general(
                    codes.astype(f32).astype(bf16),
                    hot.astype(bf16),
                    contract_lanes,
                    preferred_element_type=f32,
                )
            ids = found[0:1] * 64.0 + found[1:2] - 1.0
            gid_s[b, :, start : start + lanes] = jnp.broadcast_to(
                ids.astype(jnp.int32), (sublanes, lanes)
            )

    for k in range(chips):
        across_copy(k).wait_recv()
    if not aligned:
        for d in range(dp_count):
            w_s[d * shard : (d + 1) * shard, :] = w_slab_s[d]

    for copy in local[3:]:
        copy.wait()
    def project(i):
        at = pl.ds(pl.multiple_of(i * wide, wide), wide)
        proj = jnp.dot(mem_s[at, :], w_s[...], preferred_element_type=f32)
        key_proj = proj[:, :width]
        key_s[at, :] = key_proj
        square = jnp.sum(key_proj * key_proj, axis=1, keepdims=True)
        cross = jnp.sum(hid_s[at, :].astype(f32) * key_proj, axis=1, keepdims=True)
        output = jnp.sum(grd_s[at, :].astype(f32) * proj[:, width:], axis=1, keepdims=True)
        lane = lax.broadcasted_iota(jnp.int32, (wide, lanes), 1)
        packed = jnp.where(
            lane == 0, square, jnp.where(lane == 1, cross, jnp.where(lane == 2, output, 0.0))
        )
        sums_s[i, z] = packed.T[:sublanes, :]
        for n in range(1, t_count):
            sums_copy(i, n).start()

    def sums_copy(i, n):
        ref = sums_s.at[i, z]
        return remote(ref, ref, sum_ssem.at[i, n], sum_rsem.at[i, n], me, (z + n) % t_count)

    ahead = min(2, wides)
    for i in range(ahead):
        project(i)
    table_out[...] = jnp.zeros(table_out.shape, f32)

    def chunk_at(c):
        return pl.ds(pl.multiple_of(c * chunk, chunk), chunk)

    def part_copy(c):
        at = chunk_at(c)
        return remote(part_s.at[at], in_s.at[at], part_ssem.at[c], part_rsem.at[c], me, mate)

    def mid_copy(c):
        at = chunk_at(c)
        return remote(part_s.at[at], mid_s.at[at], mid_ssem.at[c], mid_rsem.at[c], me, other)

    def total_copy(c):
        at = chunk_at(c)
        return remote(total_s.at[at], total_s.at[at], total_ssem.at[c], total_rsem.at[c], me, mate)

    def grads(i):
        at = pl.ds(pl.multiple_of(i * tile, tile), tile)
        group = i // per_wide

        @pl.when(i % per_wide == 0)
        def _():
            for n in range(1, t_count):
                sums_copy(group, n).wait_recv()

        lane_at = pl.ds(pl.multiple_of((i % per_wide) * tile, tile), tile)
        sums = sums_s[group, 0, :, lane_at]
        for part in range(1, t_count):
            sums = sums + sums_s[group, part, :, lane_at]
        root_width = math.sqrt(model_width)
        key_scale = jnp.sqrt(sums[0:1] / model_width + norm_eps)
        gate_score = sums[1:2] / (key_scale * root_width)
        gate_value = 1.0 / (1.0 + jnp.exp(-gate_score))
        gate_grad = gate_value * (1.0 - gate_value) * sums[2:3]
        hidden_factor = gate_grad / (key_scale * root_width)
        key_factor = gate_grad * (gate_score / (model_width * key_scale * key_scale))
        row = lax.broadcasted_iota(jnp.int32, (lanes, tile), 0)
        factors = jnp.where(
            row == 0, hidden_factor, jnp.where(row == 1, key_factor, gate_value)
        ).T
        both_s[at, :width] = (
            factors[:, 0:1] * hid_s[at, :].astype(f32) - factors[:, 1:2] * key_s[at, :]
        ).astype(bf16)
        both_s[at, width:] = (factors[:, 2:3] * grd_s[at, :].astype(f32)).astype(bf16)
        part_s[at, :] = lax.dot_general(
            both_s[at, :], w_s[...], contract_lanes, preferred_element_type=f32
        ).astype(bf16)

        @pl.when(is_end)
        def _():
            for k in range(per_tile):
                part_copy(i * per_tile + k).start()

    def weight_grad(start, size):
        value = lax.dot_general(
            mem_s[:, start : start + size], both_s[...], contract_rows, preferred_element_type=f32
        ).astype(bf16)
        if aligned:
            wg_s[start : start + size, :] = value
        else:
            at = start
            while at < start + size:
                d = at // shard
                stop = min((d + 1) * shard, start + size)
                wg_slab_s[d, at - d * shard : stop - d * shard, :] = value[
                    at - start : stop - start
                ]
                at = stop

    def pair_copy(k):
        return remote(
            wg_slab(k * 2 + 1 - core), pair_s.at[k], pair_ssem.at[k], pair_rsem.at[k], partner, z
        )

    def half_copy(s, k):
        at = (1 << s) + k
        return remote(
            wg_slab(have[at] * 2 + core),
            half_s.at[at],
            half_ssem.at[at],
            half_rsem.at[at],
            flip(chip, s) * 2 + core,
            z,
        )

    def half_start(s):
        for k in range(1 << s):
            half_copy(s, k).start()

    def pair_sum():
        for k in range(chips):
            pair_copy(k).wait_recv()
        for k in range(chips):
            ref = wg_slab(k * 2 + core)
            ref[...] = (ref[...].astype(f32) + pair_s[k].astype(f32)).astype(bf16)

    def half_sum(s):
        for k in range(1 << s):
            half_copy(s, k).wait_recv()
        for k in range(1 << s):
            ref = wg_slab(have[k] * 2 + core)
            added = ref[...].astype(f32) + half_s[(1 << s) + k].astype(f32)
            if s:
                ref[...] = added.astype(bf16)
            else:
                key_out[...] = added[:, :width]
                value_out[...] = added[:, width:]

    def row_copy(b, j, i):
        return remote(
            send_s.at[b, j], got_s.at[b, me], row_ssem.at[b, i], row_rsem.at[b, i], j, z
        )

    dest_each = dp_count // 4 if dp_count % 4 == 0 else dp_count
    dest_parts = dp_count // dest_each

    def dispatch(b, part):
        def one(i, carry):
            j = (me + i) % dp_count
            slot = lax.broadcasted_iota(jnp.int32, (cap, block), 0) + j * cap
            rows = jnp.zeros((cap, row_width), f32)
            at = pl.ds(pl.multiple_of(b * block, block), block)
            for lookup in range(lookups):
                ids = slot_s[pl.ds(b, 1), lookup * block : (lookup + 1) * block]
                hot = jnp.where(slot == ids, 1.0, 0.0).astype(bf16)
                rows = rows + jnp.dot(
                    hot,
                    total_s[at, lookup * row_width : (lookup + 1) * row_width],
                    preferred_element_type=f32,
                )

            @pl.when(i < dp_count)
            def _():
                send_s[b, j] = rows.astype(bf16)
                row_copy(b, j, i).start()

            @pl.when(i == dp_count)
            def _():
                got_s[b, me] = rows.astype(bf16)

            return carry

        lax.fori_loop(1 + part * dest_each, 1 + (part + 1) * dest_each, one, 0)

    row_tile = divisor(rows_dev, (256, 128))
    step_lanes = divisor(slots, (512, 384, 256, 128))

    table_steps = rows_dev // row_tile
    table_each = table_steps // 4 if table_steps % 4 == 0 else table_steps
    table_parts = table_steps // table_each

    def combine(b, part):
        def arrived(i, carry):
            row_copy(b, (me + i) % dp_count, i).wait_recv()
            return carry

        @pl.when(part == 0)
        def _():
            lax.fori_loop(1, dp_count, arrived, 0)

        def one(r, carry):
            at = pl.ds(pl.multiple_of(r * row_tile, row_tile), row_tile)
            row = lax.broadcasted_iota(jnp.int32, (row_tile, step_lanes), 0) + r * row_tile
            rows = got_s[b].reshape(slots, row_width)
            added = table_out[at, :]
            for start in range(0, slots, step_lanes):
                hot = jnp.where(row == gid_s[b, 0:1, start : start + step_lanes], 1.0, 0.0)
                added = added + jnp.dot(
                    hot.astype(bf16), rows[start : start + step_lanes], preferred_element_type=f32
                )
            table_out[at, :] = added
            return carry

        lax.fori_loop(part * table_each, (part + 1) * table_each, one, 0)

    wg_tile = divisor(mem, (128,))
    wg_steps = mem // wg_tile
    lag = 3
    late = lag + 2
    grads_every = 2
    ids_first = 4
    wg_first = grads_every * (tiles - 1) + 1
    pair_first = wg_first + wg_steps
    half_first = pair_first + 2
    half_every = 4
    dispatch_first = per_block + late
    combine_first = dispatch_first + dest_parts + 4
    total_steps = max(
        combine_first + (blocks - 1) * per_block + table_parts,
        half_first + half_every * bits + 1,
        chunks + late,
    )

    def every(s, first, period, count, then):
        at = s - first

        @pl.when(
            jnp.logical_and(at >= 0, jnp.logical_and(at % period == 0, at < count * period))
        )
        def _():
            then(at // period)

    def step(s, carry):
        every(s, 0, grads_every, tiles, grads)
        every(s, 1, grads_every * per_wide, wides - ahead, lambda i: project(i + ahead))

        @pl.when(jnp.logical_and(is_mid, s < chunks))
        def _():
            part_copy(s).wait_recv()
            at = chunk_at(s)
            part_s[at, :] = (part_s[at, :].astype(f32) + in_s[at, :].astype(f32)).astype(bf16)
            mid_copy(s).start()

        @pl.when(jnp.logical_and(is_mid, jnp.logical_and(s >= lag, s < chunks + lag)))
        def _():
            c = s - lag
            mid_copy(c).wait_recv()
            at = chunk_at(c)
            total_s[at, :] = (part_s[at, :].astype(f32) + mid_s[at, :].astype(f32)).astype(bf16)
            total_copy(c).start()

        @pl.when(jnp.logical_and(is_end, jnp.logical_and(s >= late, s < chunks + late)))
        def _():
            total_copy(s - late).wait_recv()

        @pl.when(s == ids_first - 1)
        def _():
            for i in range(1, dp_count):
                ids_copy(i).wait_recv()
            lax.fori_loop(0, dp_count, own_slots, 0)

        for part in range(id_parts):
            every(s, ids_first + part, id_parts, blocks, lambda b, part=part: own_ids(b, part))

        for i in range(wg_steps):

            @pl.when(s == wg_first + i)
            def _(i=i):
                weight_grad(i * wg_tile, wg_tile)

        @pl.when(s == pair_first)
        def _():
            for k in range(chips):
                pair_copy(k).start()

        @pl.when(s == half_first)
        def _():
            pair_sum()
            half_start(bits - 1)

        for s_bit in range(bits - 1, -1, -1):

            @pl.when(s == half_first + half_every * (bits - s_bit))
            def _(s_bit=s_bit):
                half_sum(s_bit)
                if s_bit:
                    half_start(s_bit - 1)

        def spread(first, parts, work):
            at = s - first

            @pl.when(
                jnp.logical_and(
                    at >= 0,
                    jnp.logical_and(at % per_block < parts, at < blocks * per_block),
                )
            )
            def _():
                work(at // per_block, at % per_block)

        spread(dispatch_first, dest_parts, dispatch)
        spread(combine_first, table_parts, combine)
        return carry

    lax.fori_loop(0, total_steps, step, 0)

    for k in range(1, chips):
        s = k.bit_length() - 1
        if k - (1 << s) or s == bits - 1:
            gather_copy(s, k - (1 << s)).wait_send()
        half_copy(s, k - (1 << s)).wait_send()
    for k in range(chips):
        across_copy(k).wait_send()
        pair_copy(k).wait_send()
    for i in range(1, dp_count):
        ids_copy(i).wait_send()
    for i in range(wides):
        for n in range(1, t_count):
            sums_copy(i, n).wait_send()

    def sent(c, carry):
        @pl.when(is_end)
        def _():
            part_copy(c).wait_send()

        @pl.when(is_mid)
        def _():
            mid_copy(c).wait_send()
            total_copy(c).wait_send()

        return carry

    lax.fori_loop(0, chunks, sent, 0)

    def rows_sent(n, carry):
        b = n // (dp_count - 1)
        i = n % (dp_count - 1) + 1
        row_copy(b, (me + i) % dp_count, i).wait_send()
        return carry

    lax.fori_loop(0, blocks * (dp_count - 1), rows_sent, 0)


def adam_kernel(
    grad_ref, table_ref, first_ref, second_ref, new_table, new_first, new_second
):
    table_grad = grad_ref[...]
    first = beta_one * first_ref[...] + (1.0 - beta_one) * table_grad
    second = beta_two * second_ref[...] + (1.0 - beta_two) * table_grad * table_grad
    root = jnp.sqrt(second * (1.0 / correct_two)) + adam_eps
    new_table[...] = table_ref[...] - (learn_rate / correct_one) * first / root
    new_first[...] = first
    new_second[...] = second


def body(
    memory,
    hidden,
    grad_out,
    key_weight,
    value_weight,
    row_ids,
    embed_table,
    first_moment,
    second_moment,
):
    dp_count = lax.axis_size("dp")
    t_count = lax.axis_size("tensor")
    tokens, mem = memory.shape
    width = hidden.shape[1]
    shard = key_weight.shape[0]
    rows_dev, row_width = embed_table.shape
    lookups = row_ids.shape[1]
    block = tokens // t_count
    entries = block * lookups
    owners = dp_count * t_count
    chips = dp_count // 2
    cap = -(-max(2, 3 * entries // owners) // 16) * 16
    tile = divisor(block, (128,))
    chunk = divisor(tile, (32,))
    wide = divisor(tokens, (256, 128))
    chunks = tokens // chunk
    aligned = shard % 16 == 0
    if t_count != 4 or chips & (chips - 1) or (dp_count * cap) % lanes:
        raise ValueError("unsupported mesh")
    plan = dict(
        dp=dp_count, tensor=t_count, tokens=tokens, mem=mem, width=width, shard=shard, cap=cap,
        rows_dev=rows_dev, lookups=lookups, row_width=row_width, block=block, tile=tile,
        chunk=chunk, aligned=aligned, wide=wide,
    )
    ids = row_ids.reshape(t_count, block, lookups).transpose(0, 2, 1).reshape(t_count, entries)
    dma = pltpu.SemaphoreType.DMA
    vmem = pltpu.VMEM
    hbm = pl.BlockSpec(memory_space=pltpu.HBM)
    inside = pl.BlockSpec(memory_space=pltpu.VMEM)
    slab_rows = (1, 16, lanes) if aligned else (dp_count, shard, 2 * width)
    key_grad, value_grad, table_grad = pl.pallas_call(
        lambda *refs: step_kernel(plan, *refs),
        in_specs=[hbm] * 6,
        out_specs=[inside] * 3,
        out_shape=[
            jax.ShapeDtypeStruct((shard, width), f32),
            jax.ShapeDtypeStruct((shard, width), f32),
            jax.ShapeDtypeStruct((rows_dev, row_width), f32),
        ],
        scratch_shapes=[
            vmem((tokens, mem), bf16),
            vmem((tokens, width), bf16),
            vmem((tokens, width), bf16),
            vmem((mem, 2 * width), bf16),
            vmem(slab_rows, bf16),
            vmem((tokens, width), f32),
            vmem((tokens, 2 * width), bf16),
            vmem((tokens, mem), bf16),
            vmem((tokens, mem), bf16),
            vmem((tokens, mem), bf16),
            vmem((tokens, mem), bf16),
            vmem((tokens // wide, t_count, sublanes, wide), f32),
            vmem((dp_count + 2, t_count, entries), jnp.int32),
            vmem((2 * sublanes, entries), jnp.int32),
            vmem((dp_count + 2, t_count, entries), jnp.int32),
            vmem((t_count, sublanes, dp_count * cap), jnp.int32),
            vmem((t_count, dp_count, cap, row_width), bf16),
            vmem((t_count, dp_count, cap, row_width), bf16),
            vmem((mem, 2 * width), bf16),
            vmem(slab_rows, bf16),
            vmem((chips, shard, 2 * width), bf16),
            vmem((chips, shard, 2 * width), bf16),
            dma((6,)),
            dma((dp_count,)),
            dma((dp_count,)),
            dma((chips,)),
            dma((chips,)),
            dma((chips,)),
            dma((chips,)),
            dma((tokens // wide, t_count)),
            dma((tokens // wide, t_count)),
            dma((chunks,)),
            dma((chunks,)),
            dma((chunks,)),
            dma((chunks,)),
            dma((chunks,)),
            dma((chunks,)),
            dma((t_count, dp_count)),
            dma((t_count, dp_count)),
            dma((chips,)),
            dma((chips,)),
            dma((chips,)),
            dma((chips,)),
        ],
        compiler_params=pltpu.CompilerParams(
            collective_id=0, has_side_effects=True, vmem_limit_bytes=67043328
        ),
        name="step",
    )(memory, hidden, grad_out, key_weight, value_weight, ids)
    row_tile = divisor(rows_dev, (512, 256, 128))
    row_spec = pl.BlockSpec((row_tile, row_width), lambda i: (i, 0))
    table_shape = jax.ShapeDtypeStruct((rows_dev, row_width), f32)
    new_table, new_first, new_second = pl.pallas_call(
        adam_kernel,
        grid=(rows_dev // row_tile,),
        in_specs=[row_spec] * 4,
        out_specs=[row_spec] * 3,
        out_shape=[table_shape] * 3,
        name="adam",
    )(table_grad, embed_table, first_moment, second_moment)
    return (key_grad, value_grad, new_table, new_first, new_second)


def solution(mesh):
    return jax.shard_map(
        body,
        mesh=mesh,
        in_specs=(
            P("dp", None),
            P("dp", "tensor"),
            P("dp", "tensor"),
            P("dp", "tensor"),
            P("dp", "tensor"),
            P("dp", None),
            P(("dp", "tensor"), None),
            P(("dp", "tensor"), None),
            P(("dp", "tensor"), None),
        ),
        out_specs=(
            P("dp", "tensor"),
            P("dp", "tensor"),
            P(("dp", "tensor"), None),
            P(("dp", "tensor"), None),
            P(("dp", "tensor"), None),
        ),
        check_vma=False,
    )
```

time: 279 us -> 177 us (0.63)
  waiting for transfers between devices: 154 us -> 0 us
  Pallas kernels: 46.3 us -> 172 us
  local copies, waits for them, and re-layouts: 23.8 us -> 2.93 us
  blocking collectives: 15.5 us -> 0 us
  between operations: 13.8 us -> 0.66 us
  matrix products: 11.5 us -> 0 us
  starting transfers between devices: 8.94 us -> 0 us
  other arithmetic: 4.05 us -> 0 us
    pallas_call x4 -> x2, Pallas kernels: 46.3 us -> 172 us  [the longest x1 166 us: body(): pl.pallas_call(lambda *refs: step_kernel(plan, *refs), in_specs=[hbm] * 6...]
    reduce_scatter x1 -> x0, waiting for transfers between devices: 63.1 us -> none  [body(): total = lax.psum_scatter(pieces, 'tensor', scatter_dimension=0, tiled=True)]
    unnamed x4 -> x0, waiting for transfers between devices: 54.5 us -> none
    all_gather x1 -> x0, waiting for transfers between devices: 36.8 us -> none  [body(): lax.all_gather(jnp.concatenate([key_weight, value_weight], axis=1), 'dp',...]
    all_gather x1 -> x0, blocking collectives: 15.5 us -> none  [body(): all_sums = lax.all_gather(sums, 'tensor', axis=0)]
    dot_general x3 -> x0, matrix products: 11.5 us -> none  [the longest x1 9.49 us: body(): lax.dot_general(memory, both_grads, (((0,), (0,)), ((), ())), preferred_e...]
    unnamed x6 -> x7, local copies, waits for them, and re-layouts: 12.6 us -> 2.93 us
    all_to_all x2 -> x0, starting transfers between devices: 8.82 us -> none  [the longest x1 5.1 us: body(): lax.all_to_all(send_rows.reshape(owners, capacity, row_width), ('dp', 'te...]
  transfers between devices with their start and end apart: 5 -> 0, of which waited for: 3 -> 0; matrix products, arithmetic and copies ran while one was open for 13% -> 0% of each run, Pallas kernels for 4% -> 0%
where the time goes in v1:
time: 177 us; the launch traced here: 176 us
  Pallas kernels  172 us (97%)
  local copies, waits for them, and re-layouts  2.93 us (2%)
    pallas_call x1, Pallas kernels, body(): pl.pallas_call(lambda *refs: step_kernel(plan, *refs), in_specs=[hbm] * 6...  166 us
    pallas_call x1, Pallas kernels, body(): pl.pallas_call(adam_kernel, grid=(rows_dev // row_tile,), in_specs=[row_s...  6.47 us

profile of v1, /device:TPU:0, one launch (start us, length us, event | category | flops | bytes accessed | tf_op | source)
XLA Modules:
  0.0 175.6 jit_solution(17670322800134116003)
XLA Ops:
  0.6 1.4 copy.16
  2.0 165.6 %step.1 = (f32[160,640]{1,0:T(8,128)}, f32[160,640]{1,0:T(8,128)}, f32[2048,256]{1,0:T(8,128)}) custom-call(bf16[1536,1280]{1,0:T(8,128)(2,1)} %refs_0_.1, bf16[1536,640]{1,0:T(8,128)(2,1)} %refs_1_.1, bf16[1536,640]{1,0:T(8,128)(2,1)} %refs_2_.1, bf16[160,640]{1,0:T(8,128)(2,1)} %refs_3_.1, bf16[160,640]{1,0:T(8,128)(2,1)} %refs_4_.1, s32[4,1920]{1,0:T(4,128)} %bitcast.5), custom_call_target="tpu_custom_call" | custom-call | tf_op jit(solution)/shard_map/step/pallas_call | solution.py:665
  167.6 0.0 copy-start.1
  167.6 0.0 copy-start
  167.6 6.5 %adam.1 = (f32[2048,256]{1,0:T(8,128)}, f32[2048,256]{1,0:T(8,128)}, f32[2048,256]{1,0:T(8,128)}) custom-call(f32[2048,256]{1,0:T(8,128)} %get-tuple-element.13.grad_ref, f32[2048,256]{1,0:T(8,128)} %table_ref.1, f32[2048,256]{1,0:T(8,128)} %first_ref.1, f32[2048,256]{1,0:T(8,128)} %second_ref.1), custom_call_target="tpu_custom_call" | custom-call | tf_op jit(solution)/shard_map/adam/pallas_call | solution.py:727
  174.1 0.0 copy-done.1
  174.1 0.8 copy.19
  174.9 0.0 copy-done
  174.9 0.8 copy.20
Async XLA Ops:
  167.6 6.5 %copy-start.1 = (f32[160,640]{1,0:T(8,128)S(1)}, f32[160,640]{1,0:T(8,128)}, u32[]{:S(2)}) copy-start(f32[160,640]{1,0:T(8,128)} %get-tuple-element.22) | copy-start | bytes 1228804
  167.6 7.2 %copy-start = (f32[160,640]{1,0:T(8,128)S(1)}, f32[160,640]{1,0:T(8,128)}, u32[]{:S(2)}) copy-start(f32[160,640]{1,0:T(8,128)} %get-tuple-element.23) | copy-start | bytes 1228804

commit v2 on v1

--- a/solution.py
+++ b/solution.py
@@ -473,14 +473,14 @@
 
     wg_tile = divisor(mem, (128,))
     wg_steps = mem // wg_tile
-    lag = 3
+    lag = 4
     late = lag + 2
-    grads_every = 2
+    grads_every = 3
     ids_first = 4
     wg_first = grads_every * (tiles - 1) + 1
     pair_first = wg_first + wg_steps
     half_first = pair_first + 2
-    half_every = 4
+    half_every = 7
     dispatch_first = per_block + late
     combine_first = dispatch_first + dest_parts + 4
     total_steps = max(

time: 177 us -> 172 us (0.972)
  Pallas kernels: 172 us -> 168 us
    pallas_call x1, Pallas kernels: 166 us -> 161 us  [body(): pl.pallas_call(lambda *refs: step_kernel(plan, *refs), in_specs=[hbm] * 6...]
where the time goes in v2:
time: 172 us; the launch traced here: 171 us
  Pallas kernels  168 us (98%)
  local copies, waits for them, and re-layouts  2.93 us (2%)
    pallas_call x1, Pallas kernels, body(): pl.pallas_call(lambda *refs: step_kernel(plan, *refs), in_specs=[hbm] * 6...  161 us
    pallas_call x1, Pallas kernels, body(): pl.pallas_call(adam_kernel, grid=(rows_dev // row_tile,), in_specs=[row_s...  6.47 us

profile of v2, /device:TPU:0, one launch (start us, length us, event | category | flops | bytes accessed | tf_op | source)
XLA Modules:
  0.0 171.2 jit_solution(18056899360195343978)
XLA Ops:
  0.6 1.4 copy.16
  2.0 161.2 %step.1 = (f32[160,640]{1,0:T(8,128)}, f32[160,640]{1,0:T(8,128)}, f32[2048,256]{1,0:T(8,128)}) custom-call(bf16[1536,1280]{1,0:T(8,128)(2,1)} %refs_0_.1, bf16[1536,640]{1,0:T(8,128)(2,1)} %refs_1_.1, bf16[1536,640]{1,0:T(8,128)(2,1)} %refs_2_.1, bf16[160,640]{1,0:T(8,128)(2,1)} %refs_3_.1, bf16[160,640]{1,0:T(8,128)(2,1)} %refs_4_.1, s32[4,1920]{1,0:T(4,128)} %bitcast.5), custom_call_target="tpu_custom_call" | custom-call | tf_op jit(solution)/shard_map/step/pallas_call | solution.py:665
  163.2 0.0 copy-start.1
  163.2 0.0 copy-start
  163.2 6.5 %adam.1 = (f32[2048,256]{1,0:T(8,128)}, f32[2048,256]{1,0:T(8,128)}, f32[2048,256]{1,0:T(8,128)}) custom-call(f32[2048,256]{1,0:T(8,128)} %get-tuple-element.13.grad_ref, f32[2048,256]{1,0:T(8,128)} %table_ref.1, f32[2048,256]{1,0:T(8,128)} %first_ref.1, f32[2048,256]{1,0:T(8,128)} %second_ref.1), custom_call_target="tpu_custom_call" | custom-call | tf_op jit(solution)/shard_map/adam/pallas_call | solution.py:727
  169.7 0.0 copy-done.1
  169.7 0.8 copy.19
  170.5 0.0 copy-done
  170.5 0.8 copy.20
Async XLA Ops:
  163.2 6.5 %copy-start.1 = (f32[160,640]{1,0:T(8,128)S(1)}, f32[160,640]{1,0:T(8,128)}, u32[]{:S(2)}) copy-start(f32[160,640]{1,0:T(8,128)} %get-tuple-element.22) | copy-start | bytes 1228804
  163.2 7.2 %copy-start = (f32[160,640]{1,0:T(8,128)S(1)}, f32[160,640]{1,0:T(8,128)}, u32[]{:S(2)}) copy-start(f32[160,640]{1,0:T(8,128)} %get-tuple-element.23) | copy-start | bytes 1228804
